TPU v7x, 32 devices: a whole 2x2x4 slice. The times are simulated.
32 devices in a mesh: inst: 4 (over x, core), dp: 4 (over z), tp: 2 (over y).
Axes of the slice: x: 2, y: 2, z: 4, core: 2. Of those that a mesh axis runs over, the one named last changes fastest.
Arguments:
- kernel_grads: bfloat16 [16, 2, 128, 4608], P(('inst', 'dp'), 'tp'), may hold values from -0.75 to 0.75
- kernel_master: float32 [2, 128, 4608], P('tp', 'dp'), may hold values from -6 to 6
- kernel_first: float32 [2, 128, 4608], P('tp', 'dp'), may hold values from -3 to 3
- kernel_second: float32 [2, 128, 4608], P('tp', 'dp'), may hold values from 0.05 to 4
- gain_grads: bfloat16 [32, 4, 4608], P(('inst', 'dp', 'tp')), may hold values from -0.29882812 to 0.29882812
- gain_master: float32 [4, 4608], replicated, may hold values from -6 to 6
- gain_first: float32 [4, 4608], replicated, may hold values from -3 to 3
- gain_second: float32 [4, 4608], replicated, may hold values from 0.05 to 4
Outputs:
- kernel_params: bfloat16 [2, 128, 4608], P('tp')
- kernel_master_new: float32 [2, 128, 4608], P('tp', 'dp')
- kernel_first_new: float32 [2, 128, 4608], P('tp', 'dp')
- kernel_second_new: float32 [2, 128, 4608], P('tp', 'dp')
- gain_params: bfloat16 [4, 4608], replicated
- gain_master_new: float32 [4, 4608], replicated
- gain_first_new: float32 [4, 4608], replicated
- gain_second_new: float32 [4, 4608], replicated
All inputs are finite; a program needn't handle non-finite values.
Results may differ from a plain program's by a relative error of at most 0.004.
Values may be sent and summed in bfloat16 or wider, within the bound.
A program may use at most 64 MiB of HBM per device.

v0:
```python
import jax
import jax.numpy as jnp
from jax import lax
from jax.sharding import PartitionSpec as P

beta_one = 0.9
beta_two = 0.95
learn_rate = 0.01
decay_rate = 0.1
epsilon = 1e-08
step_count = 100.0


def adam_update(gradient, master, first_moment, second_moment):
    first_next = beta_one * first_moment + (1.0 - beta_one) * gradient
    second_next = beta_two * second_moment + (1.0 - beta_two) * gradient * gradient
    first_hat = first_next / (1.0 - beta_one**step_count)
    second_hat = second_next / (1.0 - beta_two**step_count)
    master_next = master - learn_rate * (
        first_hat / (jnp.sqrt(second_hat) + epsilon) + decay_rate * master
    )
    return (master_next, first_next, second_next)


def local(
    kernel_grads,
    kernel_master,
    kernel_first,
    kernel_second,
    gain_grads,
    gain_master,
    gain_first,
    gain_second,
):
    local_grads = kernel_grads[0].astype(jnp.float32)
    gain_local = gain_grads[0].astype(jnp.float32)
    flat_grads = gain_local.reshape(-1)
    gain_whole = None
    partial_rows, gain_piece = (
        lax.psum_scatter(
            local_grads.astype(jnp.bfloat16), "dp", scatter_dimension=1, tiled=True
        ).astype(jnp.float32),
        lax.psum_scatter(
            flat_grads.astype(jnp.bfloat16), "dp", scatter_dimension=0, tiled=True
        ).astype(jnp.float32),
    )
    gradient, gain_piece = (
        lax.psum(partial_rows.astype(jnp.bfloat16), "inst").astype(jnp.float32),
        lax.psum(gain_piece.astype(jnp.bfloat16), "inst").astype(jnp.float32),
    )
    kernel_master_new, kernel_first_new, kernel_second_new = adam_update(
        gradient, kernel_master, kernel_first, kernel_second
    )
    kernel_params = lax.all_gather(kernel_master_new.astype(jnp.bfloat16), "dp", axis=1, tiled=True)
    gain_piece = lax.psum(gain_piece, "tp")
    gain_whole = lax.all_gather(gain_piece, "dp", axis=0, tiled=True).reshape(gain_master.shape)
    gain_master_new, gain_first_new, gain_second_new = adam_update(
        gain_whole, gain_master, gain_first, gain_second
    )
    gain_params = gain_master_new.astype(jnp.bfloat16)
    return (
        kernel_params,
        kernel_master_new,
        kernel_first_new,
        kernel_second_new,
        gain_params,
        gain_master_new,
        gain_first_new,
        gain_second_new,
    )


def solution(mesh):
    return jax.shard_map(
        local,
        mesh=mesh,
        in_specs=(
            P(("inst", "dp"), "tp", None, None),
            P("tp", "dp", None),
            P("tp", "dp", None),
            P("tp", "dp", None),
            P(("inst", "dp", "tp"), None, None),
            P(),
            P(),
            P(),
        ),
        out_specs=(
            P("tp", None, None),
            P("tp", "dp", None),
            P("tp", "dp", None),
            P("tp", "dp", None),
            P(),
            P(),
            P(),
            P(),
        ),
        check_vma=False,
    )
```

profile of v0, /device:TPU:0, one launch (start us, length us, event | category | flops | bytes accessed | tf_op | source)
XLA Modules:
  0.0 142.5 jit_solution(16182226304347898728)
XLA Ops:
  7.2 0.0 copy-start.1
  7.2 0.0 copy-start
  7.2 0.0 reduce-scatter.2.cloned.1.call-start
  7.2 0.7 reduce-scatter.2.cloned.1.call-update
  7.9 0.0 all-reduce.3.cloned.1.call-start
  8.0 34.4 %reduce-scatter.2.cloned.1.call-done = bf16[1,32,4608]{2,1,0:T(8,128)(2,1)} async-done(((bf16[1,128,4608]{2,1,0:T(8,128)(2,1)}), bf16[1,32,4608]{2,1,0:T(8,128)(2,1)}) %reduce-scatter.2.cloned.1.call-update) | async-done | bytes 294928 | tf_op jit(solution)/shard_map/reduce_scatter | solution.py:40
  42.4 0.0 all-reduce.3.cloned.1.call-update
  42.4 0.0 copy-start.5
  42.4 0.0 copy-start.6
  42.4 0.0 copy-start.2
  42.4 0.0 copy-start.3
  42.5 0.0 copy-start.4
  42.5 0.0 all-gather.3.cloned.1.call-start
  42.5 33.3 %all-reduce.3.cloned.1.call-done = bf16[1,32,4608]{2,1,0:T(8,128)(2,1)} async-done(((bf16[1,32,4608]{2,1,0:T(8,128)(2,1)}), bf16[1,32,4608]{2,1,0:T(8,128)(2,1)}) %all-reduce.3.cloned.1.call-update) | async-done | bytes 294928 | tf_op jit(solution)/shard_map/psum | solution.py:48
  75.8 0.0 copy-done.1
  75.8 0.0 copy-done
  75.8 2.7 %fusion.7 = (bf16[1,32,4608]{2,1,0:T(8,128)(2,1)}, f32[1,32,4608]{2,1,0:T(8,128)}, f32[1,32,4608]{2,1,0:T(8,128)}, f32[1,32,4608]{2,1,0:T(8,128)}) fusion(f32[1,32,4608]{2,1,0:T(8,128)S(1)} %copy-done, bf16[1,32,4608]{2,1,0:T(8,128)(2,1)} %all-reduce.3.cloned.1.call-done, f32[1,32,4608]{2,1,0:T(8,128)S(1)} %copy-done.1, f32[1,32,4608]{2,1,0:T(8,128)} %param.11), kind=kLoop, calls=%fused_computation.11 | loop fusion | flops 2506752 | bytes 4128768 | tf_op jit(solution)/shard_map/convert_element_type | solution.py:54
  78.5 0.0 all-gather.3.cloned.1.call-update
  78.6 0.0 copy-done.5
  78.6 0.0 copy-done.6
  78.6 0.6 dynamic-slice
  79.9 20.5 %all-reduce = bf16[18432]{0:T(1024)(128)(2,1)S(1)} all-reduce(bf16[18432]{0:T(1024)(128)(2,1)S(1)} %squeeze.7), channel_id=3, replica_groups=mesh['inst'=4,'dp'=4,'tp'=2] {'dp'}, use_global_device_ids=true, to_apply=%region_2.0.clone | all-reduce | flops 18432 | bytes 73728
  100.4 0.1 dynamic-slice.1
  100.5 10.9 %psum.22 = bf16[4608]{0:T(1024)(128)(2,1)S(1)} all-reduce(bf16[4608]{0:T(1024)(128)(2,1)S(1)} %dynamic-slice.1), channel_id=1, replica_groups=mesh['inst'=4,'dp'=4,'tp'=2] {'inst'}, use_global_device_ids=true, to_apply=%region_3.0 | all-reduce | flops 4608 | bytes 18432 | tf_op jit(solution)/shard_map/psum | solution.py:49
  111.4 8.2 %psum.23 = f32[4608]{0:T(1024)S(1)} all-reduce(bf16[4608]{0:T(1024)(128)(2,1)S(1)} %psum.22), channel_id=1, replica_groups=mesh['inst'=4,'dp'=4,'tp'=2] {'tp'}, use_global_device_ids=true, to_apply=%region_4.0 | all-reduce | flops 4608 | bytes 27648 | tf_op jit(solution)/shard_map/psum | solution.py:55
  119.6 13.2 %all-gather = f32[4,1,4608]{2,1,0:T(1,128)S(1)} all-gather(f32[1,1,4608]{2,1,0:T(1,128)S(1)} %reshape.22), channel_id=1, replica_groups=mesh['inst'=4,'dp'=4,'tp'=2] {'dp'}, dimensions={0}, use_global_device_ids=true | all-gather | bytes 92160 | tf_op jit(solution)/shard_map/all_gather | solution.py:56
  132.8 0.0 copy-done.2
  132.8 0.0 copy-done.3
  132.8 0.0 copy-done.4
  132.8 0.8 fusion.4
  133.6 0.0 all-gather.3.cloned.1.call-done
  133.6 2.4 %copy.23 = bf16[1,128,4608]{2,1,0:T(8,128)(2,1)} copy(bf16[1,128,4608]{2,1,0:T(8,128)(2,1)} %all-gather.3.cloned.1.call-done) | data formatting | bytes 2359296
  (2 shorter events, 0.0 us)
Async XLA Ops:
  7.2 68.6 %copy-start.1 = (f32[1,32,4608]{2,1,0:T(8,128)S(1)}, f32[1,32,4608]{2,1,0:T(8,128)}, u32[]{:S(2)}) copy-start(f32[1,32,4608]{2,1,0:T(8,128)} %param.10) | copy-start | bytes 1769476
  7.2 68.6 %copy-start = (f32[1,32,4608]{2,1,0:T(8,128)S(1)}, f32[1,32,4608]{2,1,0:T(8,128)}, u32[]{:S(2)}) copy-start(f32[1,32,4608]{2,1,0:T(8,128)} %param.9) | copy-start | bytes 1769476
  7.2 35.2 %reduce-scatter.2.cloned.1.call-start = ((), (), s32[]{:S(2)}) async-start(), calls=%async_computation.1 | async-start | bytes 1474560 | tf_op jit(solution)/shard_map/reduce_scatter | solution.py:40
  7.9 67.9 %all-reduce.3.cloned.1.call-start = ((), (), s32[]{:S(2)}) async-start(), calls=%async_computation.2 | async-start | bytes 589824 | tf_op jit(solution)/shard_map/psum | solution.py:48
  42.4 36.2 %copy-start.5 = (bf16[1,4,4608]{2,1,0:T(4,128)(2,1)S(1)}, bf16[1,4,4608]{2,1,0:T(4,128)(2,1)}, u32[]{:S(2)}) copy-start(bf16[1,4,4608]{2,1,0:T(4,128)(2,1)} %param.12) | copy-start | bytes 110596
  42.4 36.2 %copy-start.6 = (u32[32]{0:T(128)S(1)}, u32[32]{0:T(128)}, u32[]{:S(2)}) copy-start(u32[32]{0:T(128)} %constant.35) | copy-start | bytes 388
  42.4 90.3 %copy-start.2 = (f32[4,4608]{1,0:T(4,128)S(1)}, f32[4,4608]{1,0:T(4,128)}, u32[]{:S(2)}) copy-start(f32[4,4608]{1,0:T(4,128)} %param.13) | copy-start | bytes 221188
  42.4 90.3 %copy-start.3 = (f32[4,4608]{1,0:T(4,128)S(1)}, f32[4,4608]{1,0:T(4,128)}, u32[]{:S(2)}) copy-start(f32[4,4608]{1,0:T(4,128)} %param.14) | copy-start | bytes 221188
  42.5 90.3 %copy-start.4 = (f32[4,4608]{1,0:T(4,128)S(1)}, f32[4,4608]{1,0:T(4,128)}, u32[]{:S(2)}) copy-start(f32[4,4608]{1,0:T(4,128)} %param.15) | copy-start | bytes 221188
  42.5 91.1 %all-gather.3.cloned.1.call-start = ((), (), s32[]{:S(2)}) async-start(), calls=%async_computation.3 | async-start | bytes 1474560 | tf_op jit(solution)/shard_map/all_gather | solution.py:54
Sparse Core Ops, SparseCore 0:
  10.3 32.0 reduce-scatter.1
  44.7 31.0 all-reduce.2
  78.7 30.9 all-gather.2
where the time goes:
time: 143 us; the launch traced here: 142 us
  waiting for transfers between devices  68.4 us (48%)
  blocking collectives  52.8 us (37%)
  between operations  14.5 us (10%)
  other arithmetic  3.55 us (2%)
  local copies, waits for them, and re-layouts  3.1 us (2%)
    reduce_scatter x1, waiting for transfers between devices, local(): lax.psum_scatter(local_grads.astype(jnp.bfloat16), 'dp', scatter_dimensio...  34.4 us
    psum x1, waiting for transfers between devices, local(): lax.psum(partial_rows.astype(jnp.bfloat16), 'inst').astype(jnp.float32)  33.3 us
    unnamed x1, blocking collectives  20.5 us
    all_gather x1, blocking collectives, local(): lax.all_gather(gain_piece, 'dp', axis=0, tiled=True)  13.2 us
    psum x1, blocking collectives, local(): lax.psum(gain_piece.astype(jnp.bfloat16), 'inst').astype(jnp.float32)  10.9 us
    psum x1, blocking collectives, local(): gain_piece = lax.psum(gain_piece, 'tp')  8.21 us
    unnamed x18, local copies, waits for them, and re-layouts  3.08 us
  transfers between devices with their start and end apart: 3, of which 2 were waited for; matrix products, arithmetic and copies ran while one was open for 1% of the time, Pallas kernels for 0%

commit v1 on v0

--- a/solution.py
+++ b/solution.py
@@ -44,9 +44,10 @@
             flat_grads.astype(jnp.bfloat16), "dp", scatter_dimension=0, tiled=True
         ).astype(jnp.float32),
     )
+    settle_edge_by_axis = lambda u_in: lax.all_gather(u_in, axis_name="inst").sum(axis=0)
     gradient, gain_piece = (
         lax.psum(partial_rows.astype(jnp.bfloat16), "inst").astype(jnp.float32),
-        lax.psum(gain_piece.astype(jnp.bfloat16), "inst").astype(jnp.float32),
+        settle_edge_by_axis(gain_piece.astype(jnp.bfloat16)).astype(jnp.float32),
     )
     kernel_master_new, kernel_first_new, kernel_second_new = adam_update(
         gradient, kernel_master, kernel_first, kernel_second

time: 143 us -> 137 us (0.958)
  blocking collectives: 52.8 us -> 47.2 us
    psum x1 -> x0, blocking collectives: 10.9 us -> none  [local(): lax.psum(gain_piece.astype(jnp.bfloat16), 'inst').astype(jnp.float32)]
    all_gather x0 -> x1, blocking collectives: none -> 5.26 us  [local(): lax.all_gather(u_in, axis_name='inst').sum(axis=0)]
    unnamed x18 -> x19, local copies, waits for them, and re-layouts: 3.08 us -> 3.09 us
where the time goes in v1:
time: 137 us
  waiting for transfers between devices  68.4 us (50%)
  blocking collectives  47.2 us (34%)
  between operations  14.5 us (11%)
  other arithmetic  3.65 us (3%)
  local copies, waits for them, and re-layouts  3.11 us (2%)
    reduce_scatter x1, waiting for transfers between devices, local(): lax.psum_scatter(local_grads.astype(jnp.bfloat16), 'dp', scatter_dimensio...  34.4 us
    psum x1, waiting for transfers between devices, local(): lax.psum(partial_rows.astype(jnp.bfloat16), 'inst').astype(jnp.float32)  33.3 us
    unnamed x1, blocking collectives  20.5 us
    all_gather x1, blocking collectives, local(): lax.all_gather(gain_piece, 'dp', axis=0, tiled=True)  13.2 us
    psum x1, blocking collectives, local(): gain_piece = lax.psum(gain_piece, 'tp')  8.22 us
    all_gather x1, blocking collectives, local(): lax.all_gather(u_in, axis_name='inst').sum(axis=0)  5.26 us
    unnamed x19, local copies, waits for them, and re-layouts  3.09 us
    convert_element_type x1, other arithmetic, local(): kernel_master_new.astype(jnp.bfloat16)  2.74 us
  transfers between devices with their start and end apart: 3, of which 2 were waited for; matrix products, arithmetic and copies ran while one was open for 1% of the time, Pallas kernels for 0%

profile of v1, /device:TPU:0, one launch (start us, length us, event | category | flops | bytes accessed | tf_op | source)
XLA Modules:
  0.0 136.9 jit_solution(10018656724080055523)
XLA Ops:
  7.2 0.0 copy-start.1
  7.2 0.0 copy-start
  7.2 0.0 reduce-scatter.2.cloned.1.call-start
  7.2 0.7 reduce-scatter.2.cloned.1.call-update
  7.9 0.0 all-reduce.3.cloned.1.call-start
  8.0 34.4 %reduce-scatter.2.cloned.1.call-done = bf16[1,32,4608]{2,1,0:T(8,128)(2,1)} async-done(((bf16[1,128,4608]{2,1,0:T(8,128)(2,1)}), bf16[1,32,4608]{2,1,0:T(8,128)(2,1)}) %reduce-scatter.2.cloned.1.call-update) | async-done | bytes 294928 | tf_op jit(solution)/shard_map/reduce_scatter | solution.py:40
  42.4 0.0 all-reduce.3.cloned.1.call-update
  42.4 0.0 copy-start.5
  42.4 0.0 copy-start.6
  42.4 0.0 copy-start.2
  42.4 0.0 copy-start.3
  42.5 0.0 copy-start.4
  42.5 0.0 all-gather.5.cloned.1.call-start
  42.5 33.3 %all-reduce.3.cloned.1.call-done = bf16[1,32,4608]{2,1,0:T(8,128)(2,1)} async-done(((bf16[1,32,4608]{2,1,0:T(8,128)(2,1)}), bf16[1,32,4608]{2,1,0:T(8,128)(2,1)}) %all-reduce.3.cloned.1.call-update) | async-done | bytes 294928 | tf_op jit(solution)/shard_map/psum | solution.py:49
  75.8 0.0 copy-done.1
  75.8 0.0 copy-done
  75.8 2.7 %fusion.7 = (bf16[1,32,4608]{2,1,0:T(8,128)(2,1)}, f32[1,32,4608]{2,1,0:T(8,128)}, f32[1,32,4608]{2,1,0:T(8,128)}, f32[1,32,4608]{2,1,0:T(8,128)}) fusion(f32[1,32,4608]{2,1,0:T(8,128)S(1)} %copy-done, bf16[1,32,4608]{2,1,0:T(8,128)(2,1)} %all-reduce.3.cloned.1.call-done, f32[1,32,4608]{2,1,0:T(8,128)S(1)} %copy-done.1, f32[1,32,4608]{2,1,0:T(8,128)} %param.11), kind=kLoop, calls=%fused_computation.11 | loop fusion | flops 2506752 | bytes 4128768 | tf_op jit(solution)/shard_map/convert_element_type | solution.py:55
  78.5 0.0 all-gather.5.cloned.1.call-update
  78.6 0.0 copy-done.5
  78.6 0.0 copy-done.6
  78.6 0.6 dynamic-slice
  79.9 20.5 %all-reduce = bf16[18432]{0:T(1024)(128)(2,1)S(1)} all-reduce(bf16[18432]{0:T(1024)(128)(2,1)S(1)} %squeeze.7), channel_id=4, replica_groups=mesh['inst'=4,'dp'=4,'tp'=2] {'dp'}, use_global_device_ids=true, to_apply=%region_2.0.clone | all-reduce | flops 18432 | bytes 73728
  100.4 0.1 dynamic-slice.1
  100.5 5.3 %all-gather.1 = bf16[4,1,4608]{2,1,0:T(2,128)(2,1)S(1)} all-gather(bf16[1,1,4608]{2,1,0:T(2,128)(2,1)S(1)} %reshape.23), channel_id=2, replica_groups=mesh['inst'=4,'dp'=4,'tp'=2] {'inst'}, dimensions={0}, use_global_device_ids=true | all-gather | bytes 46080 | tf_op jit(solution)/shard_map/all_gather | solution.py:47
  105.7 0.1 reduce_sum.12
  105.8 8.2 %psum.15 = f32[4608]{0:T(1024)S(1)} all-reduce(bf16[4608]{0:T(1024)(128)(2,1)S(1)} %reduce_sum.12), channel_id=1, replica_groups=mesh['inst'=4,'dp'=4,'tp'=2] {'tp'}, use_global_device_ids=true, to_apply=%region_4.0 | all-reduce | flops 4608 | bytes 27648 | tf_op jit(solution)/shard_map/psum | solution.py:56
  114.1 13.2 %all-gather.2 = f32[4,1,4608]{2,1,0:T(1,128)S(1)} all-gather(f32[1,1,4608]{2,1,0:T(1,128)S(1)} %reshape.25), channel_id=1, replica_groups=mesh['inst'=4,'dp'=4,'tp'=2] {'dp'}, dimensions={0}, use_global_device_ids=true | all-gather | bytes 92160 | tf_op jit(solution)/shard_map/all_gather | solution.py:57
  127.2 0.0 copy-done.2
  127.2 0.0 copy-done.3
  127.2 0.0 copy-done.4
  127.3 0.8 fusion.4
  128.1 0.0 all-gather.5.cloned.1.call-done
  128.1 2.4 %copy.23 = bf16[1,128,4608]{2,1,0:T(8,128)(2,1)} copy(bf16[1,128,4608]{2,1,0:T(8,128)(2,1)} %all-gather.5.cloned.1.call-done) | data formatting | bytes 2359296
  (3 shorter events, 0.0 us)
Async XLA Ops:
  7.2 68.6 %copy-start.1 = (f32[1,32,4608]{2,1,0:T(8,128)S(1)}, f32[1,32,4608]{2,1,0:T(8,128)}, u32[]{:S(2)}) copy-start(f32[1,32,4608]{2,1,0:T(8,128)} %param.10) | copy-start | bytes 1769476
  7.2 68.6 %copy-start = (f32[1,32,4608]{2,1,0:T(8,128)S(1)}, f32[1,32,4608]{2,1,0:T(8,128)}, u32[]{:S(2)}) copy-start(f32[1,32,4608]{2,1,0:T(8,128)} %param.9) | copy-start | bytes 1769476
  7.2 35.2 %reduce-scatter.2.cloned.1.call-start = ((), (), s32[]{:S(2)}) async-start(), calls=%async_computation.1 | async-start | bytes 1474560 | tf_op jit(solution)/shard_map/reduce_scatter | solution.py:40
  7.9 67.9 %all-reduce.3.cloned.1.call-start = ((), (), s32[]{:S(2)}) async-start(), calls=%async_computation.2 | async-start | bytes 589824 | tf_op jit(solution)/shard_map/psum | solution.py:49
  42.4 36.2 %copy-start.5 = (bf16[1,4,4608]{2,1,0:T(4,128)(2,1)S(1)}, bf16[1,4,4608]{2,1,0:T(4,128)(2,1)}, u32[]{:S(2)}) copy-start(bf16[1,4,4608]{2,1,0:T(4,128)(2,1)} %param.12) | copy-start | bytes 110596
  42.4 36.2 %copy-start.6 = (u32[32]{0:T(128)S(1)}, u32[32]{0:T(128)}, u32[]{:S(2)}) copy-start(u32[32]{0:T(128)} %constant.38) | copy-start | bytes 388
  42.4 84.8 %copy-start.2 = (f32[4,4608]{1,0:T(4,128)S(1)}, f32[4,4608]{1,0:T(4,128)}, u32[]{:S(2)}) copy-start(f32[4,4608]{1,0:T(4,128)} %param.13) | copy-start | bytes 221188
  42.4 84.8 %copy-start.3 = (f32[4,4608]{1,0:T(4,128)S(1)}, f32[4,4608]{1,0:T(4,128)}, u32[]{:S(2)}) copy-start(f32[4,4608]{1,0:T(4,128)} %param.14) | copy-start | bytes 221188
  42.5 84.8 %copy-start.4 = (f32[4,4608]{1,0:T(4,128)S(1)}, f32[4,4608]{1,0:T(4,128)}, u32[]{:S(2)}) copy-start(f32[4,4608]{1,0:T(4,128)} %param.15) | copy-start | bytes 221188
  42.5 85.6 %all-gather.5.cloned.1.call-start = ((), (), s32[]{:S(2)}) async-start(), calls=%async_computation.3 | async-start | bytes 1474560 | tf_op jit(solution)/shard_map/all_gather | solution.py:55
Sparse Core Ops, SparseCore 0:
  10.3 32.0 reduce-scatter.1
  44.7 31.0 all-reduce.2
  78.7 30.9 all-gather.4
